TPU v7x, 32 devices: a whole 2x2x4 slice. The times are simulated.
32 devices in a mesh: dp: 4 (over y, x), ctx: 8 (over z, core).
Axes of the slice: x: 2, y: 2, z: 4, core: 2. Of those that a mesh axis runs over, the one named last changes fastest.
Arguments:
- queries: bfloat16 [4096, 4096], P(('dp', 'ctx')), parts along dimension 0, may hold values from -9 to 9
- keys: bfloat16 [4096, 512], P(('dp', 'ctx')), parts along dimension 0, may hold values from -9 to 9
- values: bfloat16 [4096, 512], P(('dp', 'ctx')), parts along dimension 0, may hold values from -6 to 6
- doc_lengths: int32 [32], P('dp'), parts along dimension 0, may hold values from 1 to 512, as said below
- row_owner: int32 [4096, 1], P(('dp', 'ctx')), parts along dimension 0, may hold values from 0 to 7; in each aligned block of 128 rows (0 to 127, 128 to 255, ...) at most 24 rows name the same one
Outputs:
- handed: bfloat16 [6144, 4096], P(('dp', 'ctx')), parts along dimension 0
There are 4 independent parts, one for each index of `dp`. A program takes and returns all parts, laid end to end along the dimension named above; each array names one. Nothing has to cross between parts.
Inputs may be any that keep to these rules, and one draw needn't show every extreme that they name: `doc_lengths`: the lengths sum to 1024; the longest is exactly 512. `row_owner`: among the 128 rows of one device, no owner is named more than 24 times.
All inputs are finite; a program needn't handle non-finite values.
Results may differ from a plain program's by a relative error of at most 0.0046.
Values may be sent and summed in bfloat16 or wider, within the bound.
No kernel may reach another device: no remote copies, remote signals or barrier semaphores. Data moves between devices by JAX's collectives and lax.ppermute only.
A program may use at most 64 MiB of HBM per device.

v0:
```python
import functools
import math

import jax
import jax.numpy as jnp
from jax import lax
from jax.experimental import pallas as pl
from jax.experimental.pallas import tpu as pltpu
from jax.sharding import PartitionSpec as P

HEADS = 32
KVH = 4
HD = 128
WIN_DEV = 4

masked_score = -1e30


def shifted(block, axis, distance):
    devices = range(lax.axis_size(axis))
    route = [(i - distance, i) for i in devices if i - distance in devices]
    return lax.ppermute(block, axis, route)


def block_scores(grouped, key_part, allowed_part):
    key_heads = key_part.reshape(key_part.shape[0], grouped.shape[1], HD)
    scores = jnp.einsum(
        "tkgd,skd->kgts", grouped, key_heads, preferred_element_type=jnp.float32
    ) * (1.0 / math.sqrt(HD))
    return jnp.where(allowed_part[None, None], scores, masked_score)


def softmax_weights(scores):
    peak = jnp.max(scores, axis=-1, keepdims=True)
    weights = jnp.exp(scores - peak)
    total = jnp.sum(weights, axis=-1, keepdims=True)
    return (weights / total).astype(jnp.bfloat16)


def mix_block(probs_part, value_part):
    value_heads = value_part.reshape(value_part.shape[0], probs_part.shape[0], HD)
    return jnp.einsum("kgts,skd->tkgd", probs_part, value_heads, preferred_element_type=jnp.float32)


def doc_numbers(doc_ends, positions):
    return jnp.sum((doc_ends[None, :] <= positions[:, None]).astype(jnp.int32), axis=1)


def plain_body(queries, keys, values, doc_lengths, row_owner, slot_count):
    row_count = queries.shape[0]
    ctx_count = lax.axis_size("ctx")
    device_index = lax.axis_index("ctx")
    group_size = HEADS // KVH
    stack_keys, stack_values = (keys, values)
    reach_width = 1
    for _ in range(WIN_DEV.bit_length() - 1):
        moved_keys, moved_values = shifted((stack_keys, stack_values), "ctx", reach_width)
        stack_keys = jnp.concatenate([moved_keys, stack_keys], axis=0)
        stack_values = jnp.concatenate([moved_values, stack_values], axis=0)
        reach_width = reach_width * 2
    far_keys, far_values = shifted((keys, values), "ctx", WIN_DEV)
    window_keys = jnp.concatenate([far_keys, stack_keys], axis=0)
    window_values = jnp.concatenate([far_values, stack_values], axis=0)
    query_pos = device_index * row_count + lax.iota(jnp.int32, row_count)
    key_pos = (device_index - WIN_DEV) * row_count + lax.iota(jnp.int32, (WIN_DEV + 1) * row_count)
    doc_ends = jnp.cumsum(doc_lengths)
    query_doc = doc_numbers(doc_ends, query_pos)
    key_doc = doc_numbers(doc_ends, key_pos)
    allowed = (
        (query_doc[:, None] == key_doc[None, :])
        & (key_pos[None, :] <= query_pos[:, None])
        & (key_pos[None, :] >= 0)
    )
    grouped_all = queries.reshape(row_count, KVH, group_size, HD)
    owner_column = row_owner[:, 0]
    onehot = (owner_column[:, None] == lax.iota(jnp.int32, ctx_count)[None, :]).astype(jnp.int32)
    earlier_count = jnp.cumsum(onehot, axis=0) - onehot
    slot_rank = jnp.sum(earlier_count * onehot, axis=1)
    slot_index = owner_column * slot_count + slot_rank
    probs = softmax_weights(block_scores(grouped_all, window_keys, allowed))
    attended = mix_block(probs, window_values)
    merged = attended.reshape(row_count, HEADS * HD).astype(jnp.bfloat16)
    return lax.all_to_all(
        jnp.zeros((ctx_count * slot_count, merged.shape[1]), jnp.bfloat16)
        .at[slot_index]
        .set(merged),
        "ctx",
        split_axis=0,
        concat_axis=0,
        tiled=True,
    )


VM = pltpu.VMEM
INFO = 128
GRANT = 16 * 1024 * 1024
SPLIT = (2, 2)
DIRECT = "ab"


def pack_kernel(k_ref, v_ref, *refs):
    parts, sems = refs[:-1], refs[-1]
    copies = []
    low = 0
    for part in parts:
        wide = part.shape[1] // 2
        for n, ref in enumerate((k_ref, v_ref)):
            copies.append(
                pltpu.make_async_copy(
                    ref.at[:, low : low + wide],
                    part.at[:, n * wide : (n + 1) * wide],
                    sems.at[len(copies)],
                )
            )
        low += wide
    for copy in copies:
        copy.start()
    for copy in copies:
        copy.wait()


def order_kernel(
    slot_count,
    at_ref,
    doc_ref,
    owner_ref,
    q_ref,
    other_owner_ref,
    other_q_ref,
    qs_ref,
    info_ref,
    docs,
    owners,
    q_in,
    sems,
):
    pieces = q_in.shape[0]
    wide = q_in.shape[2]
    doc_copy = pltpu.make_async_copy(doc_ref, docs, sems.at[pieces])
    owner_copy = pltpu.make_async_copy(owner_ref, owners, sems.at[pieces + 1])
    q_copies = [
        pltpu.make_async_copy(q_ref.at[:, n * wide : (n + 1) * wide], q_in.at[n], sems.at[n])
        for n in range(pieces)
    ]
    doc_copy.start()
    owner_copy.start()
    for copy in q_copies:
        copy.start()
    doc_copy.wait()
    owner_copy.wait()
    rows = owners.shape[1]
    slots = info_ref.shape[0]
    ctx_count = slots // slot_count
    me = at_ref[0]
    core = lax.rem(me, 2)
    upper = (
        lax.broadcasted_iota(jnp.int32, (rows, rows), 0)
        < lax.broadcasted_iota(jnp.int32, (rows, rows), 1)
    ).astype(jnp.bfloat16)
    slot = lax.broadcasted_iota(jnp.int32, (slots, rows), 0)
    place = lax.broadcasted_iota(jnp.int32, (slots, rows), 1)
    picks, pos = [], None
    for owner, source in ((owners[...], core), (other_owner_ref[...], 1 - core)):
        named = lax.broadcasted_iota(jnp.int32, (ctx_count, rows), 0) == owner
        onehot = named.astype(jnp.float32)
        earlier = jnp.dot(onehot.astype(jnp.bfloat16), upper, preferred_element_type=jnp.float32)
        rank = jnp.sum(earlier * onehot, axis=0, keepdims=True).astype(jnp.int32)
        target = ((owner // 2) * 2 + source) * slot_count + rank
        pick = slot == jnp.where(lax.rem(owner, 2) == core, target, -1)
        base = (me - core + source) * rows
        found = jnp.max(jnp.where(pick, place + base, -1), axis=1, keepdims=True)
        pos = found if pos is None else jnp.maximum(pos, found)
        picks.append(jnp.where(pick, 1.0, 0.0).astype(jnp.bfloat16))
    start = jnp.zeros_like(pos)
    end = jnp.int32(0)
    for c in range(docs.shape[0]):
        end = end + docs[c]
        start = jnp.where(end <= pos, jnp.maximum(start, end), start)
    lane = lax.broadcasted_iota(jnp.int32, (slots, INFO), 1)
    info_ref[...] = jnp.where(lane == 0, start, pos)
    pick = jnp.concatenate(picks, axis=1)
    for n in range(pieces):
        q_copies[n].wait()
        for h in range(0, wide // HD, 2):
            head = n * (wide // HD) + h
            q = jnp.concatenate(
                [
                    q_in[n, :, h * HD : (h + 2) * HD],
                    other_q_ref[:, head * HD : (head + 2) * HD],
                ],
                axis=0,
            )
            q = jnp.dot(pick, q, preferred_element_type=jnp.float32)
            qs_ref[head] = q[:, :HD]
            qs_ref[head + 1] = q[:, HD:]


def attend_kernel(shift, first_head, heads, at_ref, qs_ref, info_ref, *refs):
    out_ref = refs[-1]
    me = at_ref[0]
    other = me + 1 - 2 * lax.rem(me, 2)
    rows = refs[0].shape[0]
    slot_count = out_ref.shape[0]
    chips = info_ref.shape[0] // slot_count
    here = lax.rem(me // 2 + shift, chips) * slot_count
    here = pl.ds(pl.multiple_of(here, slot_count), slot_count)
    group = HEADS // KVH
    lo = info_ref[here, 0:1]
    hi = info_ref[here, 1:2]
    biases = []
    for base in (me, other, me - 2, other - 2, me - 4, other - 4):
        key_pos = base * rows + lax.broadcasted_iota(jnp.int32, (slot_count, rows), 1)
        biases.append(jnp.where((key_pos >= lo) & (key_pos <= hi), 0.0, masked_score))
    bias = jnp.concatenate(biases, axis=1)[None]
    keep = (hi >= 0).astype(jnp.float32)[None]
    scale = math.log2(math.e) / math.sqrt(HD)
    for n, (part, place, share) in enumerate(heads):
        blocks = refs[6 * part : 6 * part + 6]
        kc = jnp.concatenate([b[:, place * HD : (place + 1) * HD] for b in blocks], axis=0)
        place += share
        vc = jnp.concatenate([b[:, place * HD : (place + 1) * HD] for b in blocks], axis=0)
        first = (first_head + n) * group
        q = qs_ref[first : first + group, here]
        q = q.reshape(group * slot_count, HD).astype(jnp.bfloat16)
        s = lax.dot_general(q, kc, (((1,), (1,)), ((), ())), preferred_element_type=jnp.float32)
        s = s.reshape(group, slot_count, s.shape[1]) * scale + bias
        p = jnp.exp2(s - jnp.max(s, axis=2, keepdims=True))
        p = p * (keep / jnp.sum(p, axis=2, keepdims=True))
        p = p.astype(jnp.bfloat16).reshape(group * slot_count, p.shape[2])
        o = jnp.dot(p, vc, preferred_element_type=jnp.float32)
        for h in range(group):
            at = (n * group + h) * HD
            out_ref[:, at : at + HD] = o[h * slot_count : (h + 1) * slot_count].astype(jnp.bfloat16)


def lay_kernel(places, at_ref, *refs):
    total = len(places)
    blocks, out_ref, sems = refs[:total], refs[total], refs[total + 1]
    chip = at_ref[0] // 2
    chips = out_ref.shape[0]
    copies = []
    for n, (shift, at) in enumerate(places):
        source = lax.rem(chip + chips - shift, chips)
        wide = blocks[n].shape[1]
        copies.append(
            pltpu.make_async_copy(blocks[n], out_ref.at[source, :, at : at + wide], sems.at[n])
        )
    for copy in copies:
        copy.start()
    for copy in copies:
        copy.wait()


def hbm():
    return pl.BlockSpec(memory_space=pltpu.HBM)


def vmem():
    return pl.BlockSpec(memory_space=VM)


def smem():
    return pl.BlockSpec(memory_space=pltpu.SMEM)


def hand_plan(count):
    chips = count // 2
    shifts = [chips // 2]
    for step in range(1, chips // 2):
        shifts += [chips // 2 - step, chips // 2 + step]
    if chips % 2:
        shifts.append(chips - 1)
    plan = [(shift, 0, SPLIT[0]) for shift in shifts]
    plan += [(shift, SPLIT[0], KVH) for shift in shifts]
    return plan + [(0, 0, KVH)]


def fits(count, rows):
    slot_count = max(3, 3 * rows // (2 * count))
    return count % 2 == 0 and count <= 16 and slot_count % 8 == 0 and rows % 128 == 0


def body(queries, keys, values, doc_lengths, row_owner):
    rows = queries.shape[0]
    count = lax.axis_size("ctx")
    slot_count = max(3, 3 * rows // (2 * count))
    if not fits(count, rows):
        return plain_body(queries, keys, values, doc_lengths, row_owner, slot_count)
    me = lax.axis_index("ctx")
    slots = count * slot_count
    width = HEADS * HD

    up = [(i, i + 2) for i in range(count - 2)]
    up_twice = [(i, i + 4) for i in range(count - 4)]
    swap = [(i, i ^ 1) for i in range(count)]
    at = jnp.full((1,), me, jnp.int32)
    params = pltpu.CompilerParams(vmem_limit_bytes=GRANT)

    def hop(block, route):
        return lax.ppermute(block, "ctx", route)

    packed = pl.pallas_call(
        pack_kernel,
        out_shape=[jax.ShapeDtypeStruct((rows, 2 * n * HD), jnp.bfloat16) for n in SPLIT],
        in_specs=[hbm(), hbm()],
        out_specs=[vmem() for n in SPLIT],
        scratch_shapes=[pltpu.SemaphoreType.DMA((2 * len(SPLIT),))],
        compiler_params=params,
        name="pack",
    )(*[pltpu.with_memory_space_constraint(part, pltpu.HBM) for part in (keys, values)])
    windows = []
    for own, tag in zip(packed, "ab"):
        near = hop(own, up)
        far = hop(own, up_twice) if tag in DIRECT else hop(near, up)
        windows.append((own, hop(own, swap), near, hop(near, swap), far, hop(far, swap)))

    owner_line = row_owner.reshape(1, rows)
    other_q = hop(queries, swap)
    other_owner = hop(owner_line, swap)
    pieces = 4
    order = pl.pallas_call(
        functools.partial(order_kernel, slot_count),
        out_shape=(
            jax.ShapeDtypeStruct((HEADS, slots, HD), jnp.float32),
            jax.ShapeDtypeStruct((slots, INFO), jnp.int32),
        ),
        in_specs=[smem(), hbm(), hbm(), hbm(), vmem(), vmem()],
        out_specs=(vmem(), vmem()),
        scratch_shapes=[
            pltpu.SMEM(doc_lengths.shape, jnp.int32),
            pltpu.VMEM((1, rows), jnp.int32),
            pltpu.VMEM((pieces, rows, width // pieces), jnp.bfloat16),
            pltpu.SemaphoreType.DMA((pieces + 2,)),
        ],
        cost_estimate=pl.CostEstimate(
            flops=4 * slots * rows * width, bytes_accessed=6 * slots * width, transcendentals=0
        ),
        compiler_params=params,
        name="order",
    )
    outside = [
        pltpu.with_memory_space_constraint(part, pltpu.HBM)
        for part in (doc_lengths, owner_line, queries)
    ]
    qs, info = order(at, *outside, other_owner, other_q)

    both = 2 * slot_count

    def attend(shift, low, high):
        share = (high - low) * (HEADS // KVH) * HD
        used = [n for n in range(2) if (low < SPLIT[0], high > SPLIT[0])[n]]
        heads = []
        for g in range(low, high):
            part = int(g >= SPLIT[0])
            heads.append((used.index(part), g - part * SPLIT[0], SPLIT[part]))
        blocks = sum([windows[n] for n in used], ())
        return pl.pallas_call(
            functools.partial(attend_kernel, shift, low, tuple(heads)),
            out_shape=jax.ShapeDtypeStruct((both, share), jnp.bfloat16),
            in_specs=[smem()] + [vmem()] * (2 + len(blocks)),
            out_specs=vmem(),
            cost_estimate=pl.CostEstimate(
                flops=4 * both * share * 6 * rows,
                bytes_accessed=3 * rows * share + 6 * both * share,
                transcendentals=both * share // HD * 6 * rows,
            ),
            compiler_params=params,
            name="attend",
        )(at, qs, info, *blocks)

    places, blocks = [], []
    for shift, low, high in hand_plan(count):
        block = attend(shift, low, high)
        if shift:
            route = [(i, (i + 2 * shift) % count) for i in range(count)]
            block = hop(block, route)
        blocks.append(block)
        places.append((shift, low * (HEADS // KVH) * HD))

    handed = pl.pallas_call(
        functools.partial(lay_kernel, tuple(places)),
        out_shape=jax.ShapeDtypeStruct((count // 2, both, width), jnp.bfloat16),
        in_specs=[smem()] + [vmem()] * len(blocks),
        out_specs=hbm(),
        scratch_shapes=[pltpu.SemaphoreType.DMA((len(blocks),))],
        cost_estimate=pl.CostEstimate(
            flops=0, bytes_accessed=4 * slots * width, transcendentals=0
        ),
        compiler_params=params,
        name="lay",
    )(at, *blocks)
    return handed.reshape(slots, width)


def solution(mesh):
    placed = (
        P(("dp", "ctx"), None),
        P(("dp", "ctx"), None),
        P(("dp", "ctx"), None),
        P("dp"),
        P(("dp", "ctx"), None),
    )

    return jax.shard_map(
        body, mesh=mesh, in_specs=placed, out_specs=P(("dp", "ctx"), None), check_vma=False
    )
```

profile of v0, /device:TPU:0, one launch (start us, length us, event | category | flops | bytes accessed | tf_op | source)
XLA Modules:
  0.0 66.8 jit_solution(3458171537815436863)
XLA Ops:
  0.0 0.5 collective-permute-start.1
  0.5 1.0 %pack.1 = (bf16[128,512]{1,0:T(8,128)(2,1)S(1)}, bf16[128,512]{1,0:T(8,128)(2,1)S(1)}) custom-call(bf16[128,512]{1,0:T(8,128)(2,1)} %k_ref.1, bf16[128,512]{1,0:T(8,128)(2,1)} %v_ref.1), custom_call_target="tpu_custom_call" | custom-call | tf_op jit(solution)/shard_map/pack/pallas_call | solution.py:302
  1.5 4.5 %collective-permute-start.11 = (bf16[128,512]{1,0:T(8,128)(2,1)S(1)}, bf16[128,512]{1,0:T(8,128)(2,1)S(1)}, u32[]{:S(2)}, u32[]{:S(2)}) collective-permute-start(bf16[128,512]{1,0:T(8,128)(2,1)S(1)} %get-tuple-element.12.refs_0_.refs_6_), channel_id=1, source_target_pairs={{0,2},{1,3},{2,4},{3,5},{4,6},{5,7},{8,10},{9,11},{10,12},{11,13},... | collective-permute-start | bytes 393224 | tf_op jit(solution)/shard_map/ppermute | solution.py:300
  6.0 4.5 %collective-permute-start.13 = (bf16[128,512]{1,0:T(8,128)(2,1)S(1)}, bf16[128,512]{1,0:T(8,128)(2,1)S(1)}, u32[]{:S(2)}, u32[]{:S(2)}) collective-permute-start(bf16[128,512]{1,0:T(8,128)(2,1)S(1)} %get-tuple-element.12.refs_0_.refs_6_), channel_id=1, source_target_pairs={{0,4},{1,5},{2,6},{3,7},{8,12},{9,13},{10,14},{11,15},{16,20},{17,... | collective-permute-start | bytes 393224 | tf_op jit(solution)/shard_map/ppermute | solution.py:300
  10.5 0.1 collective-permute-start
  10.5 1.5 %collective-permute-start.3 = (bf16[128,512]{1,0:T(8,128)(2,1)S(1)}, bf16[128,512]{1,0:T(8,128)(2,1)S(1)}, u32[]{:S(2)}, u32[]{:S(2)}) collective-permute-start(bf16[128,512]{1,0:T(8,128)(2,1)S(1)} %get-tuple-element.11.refs_0_), channel_id=1, source_target_pairs={{0,2},{1,3},{2,4},{3,5},{4,6},{5,7},{8,10},{9,11},{10,12},{11,13},... | collective-permute-start | bytes 393224 | tf_op jit(solution)/shard_map/ppermute | solution.py:300
  12.0 0.0 collective-permute-done.other_owner_ref
  12.1 1.9 %collective-permute-start.5 = (bf16[128,512]{1,0:T(8,128)(2,1)S(1)}, bf16[128,512]{1,0:T(8,128)(2,1)S(1)}, u32[]{:S(2)}, u32[]{:S(2)}) collective-permute-start(bf16[128,512]{1,0:T(8,128)(2,1)S(1)} %get-tuple-element.11.refs_0_), channel_id=1, source_target_pairs={{0,4},{1,5},{2,6},{3,7},{8,12},{9,13},{10,14},{11,15},{16,20},{17,... | collective-permute-start | bytes 393224 | tf_op jit(solution)/shard_map/ppermute | solution.py:300
  14.0 0.0 collective-permute-done.11.refs_2_.refs_8_
  14.0 0.1 collective-permute-start.10
  14.1 0.3 collective-permute-done.13.refs_4_.refs_10_
  14.4 0.2 collective-permute-start.12
  14.6 0.0 collective-permute-done.1.other_q_ref
  14.6 0.3 collective-permute-start.14
  14.9 2.2 %order.1 = (f32[32,192,128]{2,1,0:T(8,128)S(1)}, s32[192,128]{1,0:T(8,128)S(1)}) custom-call(s32[1]{0:T(128)} %bitcast.at_ref, s32[8]{0:T(128)} %doc_ref.1, s32[1,128]{1,0:T(1,128)} %bitcast.4, bf16[128,4096]{1,0:T(8,128)(2,1)} %q_ref.1, s32[1,128]{1,0:T(1,128)S(1)} %collective-permute-done.other_owner_ref, ...), custom_call_target="tpu_custom_call" | custom-call | flops 402653184 | bytes 4718592 | tf_op jit(solution)/shard_map/order/pallas_call | solution.py:345
  17.1 0.0 collective-permute-done.3.refs_2_
  17.2 0.2 collective-permute-start.2
  17.4 1.9 %collective-permute-done.5.refs_4_ = bf16[128,512]{1,0:T(8,128)(2,1)S(1)} collective-permute-done((bf16[128,512]{1,0:T(8,128)(2,1)S(1)}, bf16[128,512]{1,0:T(8,128)(2,1)S(1)}, u32[]{:S(2)}, u32[]{:S(2)}) %collective-permute-start.5) | collective-permute-done | bytes 131104 | tf_op jit(solution)/shard_map/ppermute | solution.py:300
  19.3 0.0 collective-permute-start.4
  19.3 0.0 collective-permute-done.10.refs_1_.refs_7_
  19.3 0.5 collective-permute-start.6
  19.8 0.0 collective-permute-done.12.refs_3_.refs_9_
  19.8 0.0 collective-permute-done.14.refs_5_.refs_11_
  19.8 1.7 %attend.12 = bf16[48,2048]{1,0:T(8,128)(2,1)S(1)} custom-call(s32[1]{0:T(128)} %bitcast.at_ref, f32[32,192,128]{2,1,0:T(8,128)S(1)} %get-tuple-element.9.qs_ref, s32[192,128]{1,0:T(8,128)S(1)} %get-tuple-element.10.info_ref, bf16[128,512]{1,0:T(8,128)(2,1)S(1)} %get-tuple-element.12.refs_0_.refs_6_, ...), custom_call_target="tpu_custom_call" | custom-call | flops 301989888 | bytes 1376256 | tf_op jit(solution)/shard_map/attend/pallas_call | solution.py:357
  21.5 8.6 %collective-permute-start.17 = (bf16[48,2048]{1,0:T(8,128)(2,1)S(1)}, bf16[48,2048]{1,0:T(8,128)(2,1)S(1)}, u32[]{:S(2)}, u32[]{:S(2)}) collective-permute-start(bf16[48,2048]{1,0:T(8,128)(2,1)S(1)} %attend.12), channel_id=1, source_target_pairs={{0,6},{1,7},{2,0},{3,1},{4,2},{5,3},{6,4},{7,5},{8,14},{9,15},{10,... | collective-permute-start | bytes 589832 | tf_op jit(solution)/shard_map/ppermute | solution.py:300
  30.0 1.7 %attend.11 = bf16[48,2048]{1,0:T(8,128)(2,1)S(1)} custom-call(s32[1]{0:T(128)} %bitcast.at_ref, f32[32,192,128]{2,1,0:T(8,128)S(1)} %get-tuple-element.9.qs_ref, s32[192,128]{1,0:T(8,128)S(1)} %get-tuple-element.10.info_ref, bf16[128,512]{1,0:T(8,128)(2,1)S(1)} %get-tuple-element.12.refs_0_.refs_6_, ...), custom_call_target="tpu_custom_call" | custom-call | flops 301989888 | bytes 1376256 | tf_op jit(solution)/shard_map/attend/pallas_call | solution.py:357
  31.7 0.1 collective-permute-start.16
  31.8 1.7 %attend.10 = bf16[48,2048]{1,0:T(8,128)(2,1)S(1)} custom-call(s32[1]{0:T(128)} %bitcast.at_ref, f32[32,192,128]{2,1,0:T(8,128)S(1)} %get-tuple-element.9.qs_ref, s32[192,128]{1,0:T(8,128)S(1)} %get-tuple-element.10.info_ref, bf16[128,512]{1,0:T(8,128)(2,1)S(1)} %get-tuple-element.12.refs_0_.refs_6_, ...), custom_call_target="tpu_custom_call" | custom-call | flops 301989888 | bytes 1376256 | tf_op jit(solution)/shard_map/attend/pallas_call | solution.py:357
  33.4 0.0 collective-permute-done.2.refs_1_
  33.4 0.6 collective-permute-start.15
  34.1 0.0 collective-permute-done.4.refs_3_
  34.1 0.0 collective-permute-done.6.refs_5_
  34.1 1.7 %attend.9 = bf16[48,2048]{1,0:T(8,128)(2,1)S(1)} custom-call(s32[1]{0:T(128)} %bitcast.at_ref, f32[32,192,128]{2,1,0:T(8,128)S(1)} %get-tuple-element.9.qs_ref, s32[192,128]{1,0:T(8,128)S(1)} %get-tuple-element.10.info_ref, bf16[128,512]{1,0:T(8,128)(2,1)S(1)} %get-tuple-element.11.refs_0_, bf16[128,512]{1,0:T(8,128)(2,1)S(1)} %collective-permute-done.2.refs_1_, ...), custom_call_target="tpu_custom_call" | custom-call | flops 301989888 | bytes 1376256 | tf_op jit(solution)/shard_map/attend/pallas_call | solution.py:357
  35.8 3.3 %collective-permute-start.9 = (bf16[48,2048]{1,0:T(8,128)(2,1)S(1)}, bf16[48,2048]{1,0:T(8,128)(2,1)S(1)}, u32[]{:S(2)}, u32[]{:S(2)}) collective-permute-start(bf16[48,2048]{1,0:T(8,128)(2,1)S(1)} %attend.9), channel_id=1, source_target_pairs={{0,6},{1,7},{2,0},{3,1},{4,2},{5,3},{6,4},{7,5},{8,14},{9,15},{10,... | collective-permute-start | bytes 589832 | tf_op jit(solution)/shard_map/ppermute | solution.py:300
  39.1 1.7 %attend.8 = bf16[48,2048]{1,0:T(8,128)(2,1)S(1)} custom-call(s32[1]{0:T(128)} %bitcast.at_ref, f32[32,192,128]{2,1,0:T(8,128)S(1)} %get-tuple-element.9.qs_ref, s32[192,128]{1,0:T(8,128)S(1)} %get-tuple-element.10.info_ref, bf16[128,512]{1,0:T(8,128)(2,1)S(1)} %get-tuple-element.11.refs_0_, bf16[128,512]{1,0:T(8,128)(2,1)S(1)} %collective-permute-done.2.refs_1_, ...), custom_call_target="tpu_custom_call" | custom-call | flops 301989888 | bytes 1376256 | tf_op jit(solution)/shard_map/attend/pallas_call | solution.py:357
  40.8 0.8 %collective-permute-start.8 = (bf16[48,2048]{1,0:T(8,128)(2,1)S(1)}, bf16[48,2048]{1,0:T(8,128)(2,1)S(1)}, u32[]{:S(2)}, u32[]{:S(2)}) collective-permute-start(bf16[48,2048]{1,0:T(8,128)(2,1)S(1)} %attend.8), channel_id=1, source_target_pairs={{0,2},{1,3},{2,4},{3,5},{4,6},{5,7},{6,0},{7,1},{8,10},{9,11},{10,... | collective-permute-start | bytes 589832 | tf_op jit(solution)/shard_map/ppermute | solution.py:300
  41.5 1.7 %attend.7 = bf16[48,2048]{1,0:T(8,128)(2,1)S(1)} custom-call(s32[1]{0:T(128)} %bitcast.at_ref, f32[32,192,128]{2,1,0:T(8,128)S(1)} %get-tuple-element.9.qs_ref, s32[192,128]{1,0:T(8,128)S(1)} %get-tuple-element.10.info_ref, bf16[128,512]{1,0:T(8,128)(2,1)S(1)} %get-tuple-element.11.refs_0_, bf16[128,512]{1,0:T(8,128)(2,1)S(1)} %collective-permute-done.2.refs_1_, ...), custom_call_target="tpu_custom_call" | custom-call | flops 301989888 | bytes 1376256 | tf_op jit(solution)/shard_map/attend/pallas_call | solution.py:357
  43.2 0.0 collective-permute-done.17.refs_5_
  43.2 1.5 %collective-permute-start.7 = (bf16[48,2048]{1,0:T(8,128)(2,1)S(1)}, bf16[48,2048]{1,0:T(8,128)(2,1)S(1)}, u32[]{:S(2)}, u32[]{:S(2)}) collective-permute-start(bf16[48,2048]{1,0:T(8,128)(2,1)S(1)} %attend.7), channel_id=1, source_target_pairs={{0,4},{1,5},{2,6},{3,7},{4,0},{5,1},{6,2},{7,3},{8,12},{9,13},{10,... | collective-permute-start | bytes 589832 | tf_op jit(solution)/shard_map/ppermute | solution.py:300
  44.8 2.7 %attend.13.refs_6_ = bf16[48,4096]{1,0:T(8,128)(2,1)S(1)} custom-call(s32[1]{0:T(128)} %bitcast.at_ref, f32[32,192,128]{2,1,0:T(8,128)S(1)} %get-tuple-element.9.qs_ref, s32[192,128]{1,0:T(8,128)S(1)} %get-tuple-element.10.info_ref, bf16[128,512]{1,0:T(8,128)(2,1)S(1)} %get-tuple-element.11.refs_0_, bf16[128,512]{1,0:T(8,128)(2,1)S(1)} %collective-permute-done.2.refs_1_, ...), custom_call_target="tpu_custom_call" | custom-call | flops 603979776 | bytes 2752512 | tf_op jit(solution)/shard_map/attend/pallas_call | solution.py:357
  47.4 0.0 collective-permute-done.16.refs_4_
  47.4 2.5 %collective-permute-done.15.refs_3_ = bf16[48,2048]{1,0:T(8,128)(2,1)S(1)} collective-permute-done((bf16[48,2048]{1,0:T(8,128)(2,1)S(1)}, bf16[48,2048]{1,0:T(8,128)(2,1)S(1)}, u32[]{:S(2)}, u32[]{:S(2)}) %collective-permute-start.15) | collective-permute-done | bytes 196640 | tf_op jit(solution)/shard_map/ppermute | solution.py:300
  49.9 2.1 %collective-permute-done.9.refs_2_ = bf16[48,2048]{1,0:T(8,128)(2,1)S(1)} collective-permute-done((bf16[48,2048]{1,0:T(8,128)(2,1)S(1)}, bf16[48,2048]{1,0:T(8,128)(2,1)S(1)}, u32[]{:S(2)}, u32[]{:S(2)}) %collective-permute-start.9) | collective-permute-done | bytes 196640 | tf_op jit(solution)/shard_map/ppermute | solution.py:300
  52.0 2.1 %collective-permute-done.8.refs_1_ = bf16[48,2048]{1,0:T(8,128)(2,1)S(1)} collective-permute-done((bf16[48,2048]{1,0:T(8,128)(2,1)S(1)}, bf16[48,2048]{1,0:T(8,128)(2,1)S(1)}, u32[]{:S(2)}, u32[]{:S(2)}) %collective-permute-start.8) | collective-permute-done | bytes 196640 | tf_op jit(solution)/shard_map/ppermute | solution.py:300
  54.1 11.3 %collective-permute-done.7.refs_0_ = bf16[48,2048]{1,0:T(8,128)(2,1)S(1)} collective-permute-done((bf16[48,2048]{1,0:T(8,128)(2,1)S(1)}, bf16[48,2048]{1,0:T(8,128)(2,1)S(1)}, u32[]{:S(2)}, u32[]{:S(2)}) %collective-permute-start.7) | collective-permute-done | bytes 196640 | tf_op jit(solution)/shard_map/ppermute | solution.py:300
  65.4 1.2 %lay.1 = bf16[4,48,4096]{2,1,0:T(8,128)(2,1)} custom-call(s32[1]{0:T(128)} %bitcast.at_ref, bf16[48,2048]{1,0:T(8,128)(2,1)S(1)} %collective-permute-done.7.refs_0_, bf16[48,2048]{1,0:T(8,128)(2,1)S(1)} %collective-permute-done.8.refs_1_, bf16[48,2048]{1,0:T(8,128)(2,1)S(1)} %collective-permute-done.9.refs_2_, ...), custom_call_target="tpu_custom_call" | custom-call | bytes 3145728 | tf_op jit(solution)/shard_map/lay/pallas_call | solution.py:380
Async XLA Ops:
  0.0 14.6 %collective-permute-start.1 = (bf16[128,4096]{1,0:T(8,128)(2,1)}, bf16[128,4096]{1,0:T(8,128)(2,1)S(1)}, u32[]{:S(2)}, u32[]{:S(2)}) collective-permute-start(bf16[128,4096]{1,0:T(8,128)(2,1)} %q_ref.1), channel_id=1, source_target_pairs={{0,1},{1,0},{2,3},{3,2},{4,5},{5,4},{6,7},{7,6},{8,9},{9,8},{10,11... | collective-permute-start | bytes 3145736 | tf_op jit(solution)/shard_map/ppermute | solution.py:300
  1.5 12.5 %collective-permute-start.11 = (bf16[128,512]{1,0:T(8,128)(2,1)S(1)}, bf16[128,512]{1,0:T(8,128)(2,1)S(1)}, u32[]{:S(2)}, u32[]{:S(2)}) collective-permute-start(bf16[128,512]{1,0:T(8,128)(2,1)S(1)} %get-tuple-element.12.refs_0_.refs_6_), channel_id=1, source_target_pairs={{0,2},{1,3},{2,4},{3,5},{4,6},{5,7},{8,10},{9,11},{10,12},{11,13},... | collective-permute-start | bytes 393224 | tf_op jit(solution)/shard_map/ppermute | solution.py:300
  6.0 8.4 %collective-permute-start.13 = (bf16[128,512]{1,0:T(8,128)(2,1)S(1)}, bf16[128,512]{1,0:T(8,128)(2,1)S(1)}, u32[]{:S(2)}, u32[]{:S(2)}) collective-permute-start(bf16[128,512]{1,0:T(8,128)(2,1)S(1)} %get-tuple-element.12.refs_0_.refs_6_), channel_id=1, source_target_pairs={{0,4},{1,5},{2,6},{3,7},{8,12},{9,13},{10,14},{11,15},{16,20},{17,... | collective-permute-start | bytes 393224 | tf_op jit(solution)/shard_map/ppermute | solution.py:300
  10.5 1.6 %collective-permute-start = (s32[1,128]{1,0:T(1,128)}, s32[1,128]{1,0:T(1,128)S(1)}, u32[]{:S(2)}, u32[]{:S(2)}) collective-permute-start(s32[1,128]{1,0:T(1,128)} %bitcast.3), channel_id=1, source_target_pairs={{0,1},{1,0},{2,3},{3,2},{4,5},{5,4},{6,7},{7,6},{8,9},{9,8},{10,11... | collective-permute-start | bytes 1544 | tf_op jit(solution)/shard_map/ppermute | solution.py:300
  10.5 6.6 %collective-permute-start.3 = (bf16[128,512]{1,0:T(8,128)(2,1)S(1)}, bf16[128,512]{1,0:T(8,128)(2,1)S(1)}, u32[]{:S(2)}, u32[]{:S(2)}) collective-permute-start(bf16[128,512]{1,0:T(8,128)(2,1)S(1)} %get-tuple-element.11.refs_0_), channel_id=1, source_target_pairs={{0,2},{1,3},{2,4},{3,5},{4,6},{5,7},{8,10},{9,11},{10,12},{11,13},... | collective-permute-start | bytes 393224 | tf_op jit(solution)/shard_map/ppermute | solution.py:300
  12.1 7.2 %collective-permute-start.5 = (bf16[128,512]{1,0:T(8,128)(2,1)S(1)}, bf16[128,512]{1,0:T(8,128)(2,1)S(1)}, u32[]{:S(2)}, u32[]{:S(2)}) collective-permute-start(bf16[128,512]{1,0:T(8,128)(2,1)S(1)} %get-tuple-element.11.refs_0_), channel_id=1, source_target_pairs={{0,4},{1,5},{2,6},{3,7},{8,12},{9,13},{10,14},{11,15},{16,20},{17,... | collective-permute-start | bytes 393224 | tf_op jit(solution)/shard_map/ppermute | solution.py:300
  14.0 5.3 %collective-permute-start.10 = (bf16[128,512]{1,0:T(8,128)(2,1)S(1)}, bf16[128,512]{1,0:T(8,128)(2,1)S(1)}, u32[]{:S(2)}, u32[]{:S(2)}) collective-permute-start(bf16[128,512]{1,0:T(8,128)(2,1)S(1)} %get-tuple-element.12.refs_0_.refs_6_), channel_id=1, source_target_pairs={{0,1},{1,0},{2,3},{3,2},{4,5},{5,4},{6,7},{7,6},{8,9},{9,8},{10,11... | collective-permute-start | bytes 393224 | tf_op jit(solution)/shard_map/ppermute | solution.py:300
  14.4 5.4 %collective-permute-start.12 = (bf16[128,512]{1,0:T(8,128)(2,1)S(1)}, bf16[128,512]{1,0:T(8,128)(2,1)S(1)}, u32[]{:S(2)}, u32[]{:S(2)}) collective-permute-start(bf16[128,512]{1,0:T(8,128)(2,1)S(1)} %collective-permute-done.11.refs_2_.refs_8_), channel_id=1, source_target_pairs={{0,1},{1,0},{2,3},{3,2},{4,5},{5,4},{6,7},{7,6},{8,9},{9,8},{10,11... | collective-permute-start | bytes 393224 | tf_op jit(solution)/shard_map/ppermute | solution.py:300
  14.6 5.2 %collective-permute-start.14 = (bf16[128,512]{1,0:T(8,128)(2,1)S(1)}, bf16[128,512]{1,0:T(8,128)(2,1)S(1)}, u32[]{:S(2)}, u32[]{:S(2)}) collective-permute-start(bf16[128,512]{1,0:T(8,128)(2,1)S(1)} %collective-permute-done.13.refs_4_.refs_10_), channel_id=1, source_target_pairs={{0,1},{1,0},{2,3},{3,2},{4,5},{5,4},{6,7},{7,6},{8,9},{9,8},{10,11... | collective-permute-start | bytes 393224 | tf_op jit(solution)/shard_map/ppermute | solution.py:300
  17.2 16.3 %collective-permute-start.2 = (bf16[128,512]{1,0:T(8,128)(2,1)S(1)}, bf16[128,512]{1,0:T(8,128)(2,1)S(1)}, u32[]{:S(2)}, u32[]{:S(2)}) collective-permute-start(bf16[128,512]{1,0:T(8,128)(2,1)S(1)} %get-tuple-element.11.refs_0_), channel_id=1, source_target_pairs={{0,1},{1,0},{2,3},{3,2},{4,5},{5,4},{6,7},{7,6},{8,9},{9,8},{10,11... | collective-permute-start | bytes 393224 | tf_op jit(solution)/shard_map/ppermute | solution.py:300
  19.3 14.8 %collective-permute-start.4 = (bf16[128,512]{1,0:T(8,128)(2,1)S(1)}, bf16[128,512]{1,0:T(8,128)(2,1)S(1)}, u32[]{:S(2)}, u32[]{:S(2)}) collective-permute-start(bf16[128,512]{1,0:T(8,128)(2,1)S(1)} %collective-permute-done.3.refs_2_), channel_id=1, source_target_pairs={{0,1},{1,0},{2,3},{3,2},{4,5},{5,4},{6,7},{7,6},{8,9},{9,8},{10,11... | collective-permute-start | bytes 393224 | tf_op jit(solution)/shard_map/ppermute | solution.py:300
  19.3 14.8 %collective-permute-start.6 = (bf16[128,512]{1,0:T(8,128)(2,1)S(1)}, bf16[128,512]{1,0:T(8,128)(2,1)S(1)}, u32[]{:S(2)}, u32[]{:S(2)}) collective-permute-start(bf16[128,512]{1,0:T(8,128)(2,1)S(1)} %collective-permute-done.5.refs_4_), channel_id=1, source_target_pairs={{0,1},{1,0},{2,3},{3,2},{4,5},{5,4},{6,7},{7,6},{8,9},{9,8},{10,11... | collective-permute-start | bytes 393224 | tf_op jit(solution)/shard_map/ppermute | solution.py:300
  21.5 21.8 %collective-permute-start.17 = (bf16[48,2048]{1,0:T(8,128)(2,1)S(1)}, bf16[48,2048]{1,0:T(8,128)(2,1)S(1)}, u32[]{:S(2)}, u32[]{:S(2)}) collective-permute-start(bf16[48,2048]{1,0:T(8,128)(2,1)S(1)} %attend.12), channel_id=1, source_target_pairs={{0,6},{1,7},{2,0},{3,1},{4,2},{5,3},{6,4},{7,5},{8,14},{9,15},{10,... | collective-permute-start | bytes 589832 | tf_op jit(solution)/shard_map/ppermute | solution.py:300
  31.7 15.7 %collective-permute-start.16 = (bf16[48,2048]{1,0:T(8,128)(2,1)S(1)}, bf16[48,2048]{1,0:T(8,128)(2,1)S(1)}, u32[]{:S(2)}, u32[]{:S(2)}) collective-permute-start(bf16[48,2048]{1,0:T(8,128)(2,1)S(1)} %attend.11), channel_id=1, source_target_pairs={{0,2},{1,3},{2,4},{3,5},{4,6},{5,7},{6,0},{7,1},{8,10},{9,11},{10,... | collective-permute-start | bytes 589832 | tf_op jit(solution)/shard_map/ppermute | solution.py:300
  33.4 16.4 %collective-permute-start.15 = (bf16[48,2048]{1,0:T(8,128)(2,1)S(1)}, bf16[48,2048]{1,0:T(8,128)(2,1)S(1)}, u32[]{:S(2)}, u32[]{:S(2)}) collective-permute-start(bf16[48,2048]{1,0:T(8,128)(2,1)S(1)} %attend.10), channel_id=1, source_target_pairs={{0,4},{1,5},{2,6},{3,7},{4,0},{5,1},{6,2},{7,3},{8,12},{9,13},{10,... | collective-permute-start | bytes 589832 | tf_op jit(solution)/shard_map/ppermute | solution.py:300
  35.8 16.3 %collective-permute-start.9 = (bf16[48,2048]{1,0:T(8,128)(2,1)S(1)}, bf16[48,2048]{1,0:T(8,128)(2,1)S(1)}, u32[]{:S(2)}, u32[]{:S(2)}) collective-permute-start(bf16[48,2048]{1,0:T(8,128)(2,1)S(1)} %attend.9), channel_id=1, source_target_pairs={{0,6},{1,7},{2,0},{3,1},{4,2},{5,3},{6,4},{7,5},{8,14},{9,15},{10,... | collective-permute-start | bytes 589832 | tf_op jit(solution)/shard_map/ppermute | solution.py:300
  40.8 13.3 %collective-permute-start.8 = (bf16[48,2048]{1,0:T(8,128)(2,1)S(1)}, bf16[48,2048]{1,0:T(8,128)(2,1)S(1)}, u32[]{:S(2)}, u32[]{:S(2)}) collective-permute-start(bf16[48,2048]{1,0:T(8,128)(2,1)S(1)} %attend.8), channel_id=1, source_target_pairs={{0,2},{1,3},{2,4},{3,5},{4,6},{5,7},{6,0},{7,1},{8,10},{9,11},{10,... | collective-permute-start | bytes 589832 | tf_op jit(solution)/shard_map/ppermute | solution.py:300
  43.2 22.2 %collective-permute-start.7 = (bf16[48,2048]{1,0:T(8,128)(2,1)S(1)}, bf16[48,2048]{1,0:T(8,128)(2,1)S(1)}, u32[]{:S(2)}, u32[]{:S(2)}) collective-permute-start(bf16[48,2048]{1,0:T(8,128)(2,1)S(1)} %attend.7), channel_id=1, source_target_pairs={{0,4},{1,5},{2,6},{3,7},{4,0},{5,1},{6,2},{7,3},{8,12},{9,13},{10,... | collective-permute-start | bytes 589832 | tf_op jit(solution)/shard_map/ppermute | solution.py:300
where the time goes:
time: 67 us; the launch traced here: 66.8 us
  starting transfers between devices  29.2 us (44%)
  waiting for transfers between devices  20.2 us (30%)
  Pallas kernels  17.1 us (26%)
    ppermute x18, starting transfers between devices, hop(): return lax.ppermute(block, 'ctx', route)  29.2 us
    ppermute x18, waiting for transfers between devices, hop(): return lax.ppermute(block, 'ctx', route)  20.2 us
    pallas_call x7, Pallas kernels, attend(): pl.pallas_call(functools.partial(attend_kernel, shift, low, tuple(heads))...  12.7 us
    pallas_call x1, Pallas kernels, body(): qs, info = order(at, *outside, other_owner, other_q)  2.24 us
  transfers between devices with their start and end apart: 18, of which 6 were waited for; matrix products, arithmetic and copies ran while one was open for 0% of the time, Pallas kernels for 24%

commit v1 on v0

--- a/solution.py
+++ b/solution.py
@@ -233,9 +233,9 @@
             out_ref[:, at : at + HD] = o[h * slot_count : (h + 1) * slot_count].astype(jnp.bfloat16)
 
 
-def lay_kernel(places, at_ref, *refs):
+def lay_kernel(places, onto, at_ref, *refs):
     total = len(places)
-    blocks, out_ref, sems = refs[:total], refs[total], refs[total + 1]
+    blocks, out_ref, sems = refs[:total], refs[total + onto], refs[total + onto + 1]
     chip = at_ref[0] // 2
     chips = out_ref.shape[0]
     copies = []
@@ -377,18 +377,27 @@
         blocks.append(block)
         places.append((shift, low * (HEADS // KVH) * HD))
 
-    handed = pl.pallas_call(
-        functools.partial(lay_kernel, tuple(places)),
-        out_shape=jax.ShapeDtypeStruct((count // 2, both, width), jnp.bfloat16),
-        in_specs=[smem()] + [vmem()] * len(blocks),
-        out_specs=hbm(),
-        scratch_shapes=[pltpu.SemaphoreType.DMA((len(blocks),))],
-        cost_estimate=pl.CostEstimate(
-            flops=0, bytes_accessed=4 * slots * width, transcendentals=0
-        ),
-        compiler_params=params,
-        name="lay",
-    )(at, *blocks)
+    shape = jax.ShapeDtypeStruct((count // 2, both, width), jnp.bfloat16)
+
+    def lay(picked, handed):
+        chosen = [blocks[n] for n in picked]
+        return pl.pallas_call(
+            functools.partial(lay_kernel, tuple(places[n] for n in picked), handed is not None),
+            out_shape=shape,
+            in_specs=[smem()] + [vmem()] * len(chosen) + [hbm()] * (handed is not None),
+            out_specs=hbm(),
+            scratch_shapes=[pltpu.SemaphoreType.DMA((len(chosen),))],
+            input_output_aliases={1 + len(chosen): 0} if handed is not None else {},
+            cost_estimate=pl.CostEstimate(
+                flops=0, bytes_accessed=4 * slots * width, transcendentals=0
+            ),
+            compiler_params=params,
+            name="lay",
+        )(at, *chosen, *([handed] if handed is not None else []))
+
+    sends = len(blocks) - 1
+    handed = lay(list(range(sends - 2)) + [sends], None)
+    handed = lay(list(range(sends - 2, sends)), handed)
     return handed.reshape(slots, width)
 
 

time: 67 us -> 66.2 us (0.988)
  starting transfers between devices: 29.2 us -> 27.6 us
    ppermute x18, starting transfers between devices: 29.2 us -> 27.6 us  [hop(): return lax.ppermute(block, 'ctx', route)]
    pallas_call x1 -> x2, Pallas kernels: 1.19 us -> 1.82 us  [lay(): pl.pallas_call(functools.partial(lay_kernel, tuple((places[n] for n in pi...]
  transfers between devices with their start and end apart: 18 -> 18, of which waited for: 6 -> 6; matrix products, arithmetic and copies ran while one was open for 0% -> 0% of each run, Pallas kernels for 24% -> 26%
where the time goes in v1:
time: 66.2 us; the launch traced here: 65.5 us
  starting transfers between devices  27.6 us (42%)
  waiting for transfers between devices  19.9 us (30%)
  Pallas kernels  17.7 us (27%)
    ppermute x18, starting transfers between devices, hop(): return lax.ppermute(block, 'ctx', route)  27.6 us
    ppermute x18, waiting for transfers between devices, hop(): return lax.ppermute(block, 'ctx', route)  19.9 us
    pallas_call x7, Pallas kernels, attend(): pl.pallas_call(functools.partial(attend_kernel, shift, low, tuple(heads))...  12.6 us
    pallas_call x1, Pallas kernels, body(): qs, info = order(at, *outside, other_owner, other_q)  2.24 us
    pallas_call x2, Pallas kernels, lay(): pl.pallas_call(functools.partial(lay_kernel, tuple((places[n] for n in pi...  1.82 us
  transfers between devices with their start and end apart: 18, of which 6 were waited for; matrix products, arithmetic and copies ran while one was open for 0% of the time, Pallas kernels for 26%

profile of v1, /device:TPU:0, one launch (start us, length us, event | category | flops | bytes accessed | tf_op | source)
XLA Modules:
  0.0 65.5 jit_solution(8480723623822425420)
XLA Ops:
  0.0 0.5 collective-permute-start.1
  0.5 1.0 %pack.1 = (bf16[128,512]{1,0:T(8,128)(2,1)S(1)}, bf16[128,512]{1,0:T(8,128)(2,1)S(1)}) custom-call(bf16[128,512]{1,0:T(8,128)(2,1)} %k_ref.1, bf16[128,512]{1,0:T(8,128)(2,1)} %v_ref.1), custom_call_target="tpu_custom_call" | custom-call | tf_op jit(solution)/shard_map/pack/pallas_call | solution.py:302
  1.5 5.5 %collective-permute-start.5 = (bf16[128,512]{1,0:T(8,128)(2,1)S(1)}, bf16[128,512]{1,0:T(8,128)(2,1)S(1)}, u32[]{:S(2)}, u32[]{:S(2)}) collective-permute-start(bf16[128,512]{1,0:T(8,128)(2,1)S(1)} %get-tuple-element.11.refs_0_.refs_6_), channel_id=1, source_target_pairs={{0,4},{1,5},{2,6},{3,7},{8,12},{9,13},{10,14},{11,15},{16,20},{17,... | collective-permute-start | bytes 393224 | tf_op jit(solution)/shard_map/ppermute | solution.py:300
  7.0 1.3 %collective-permute-start.12 = (bf16[128,512]{1,0:T(8,128)(2,1)S(1)}, bf16[128,512]{1,0:T(8,128)(2,1)S(1)}, u32[]{:S(2)}, u32[]{:S(2)}) collective-permute-start(bf16[128,512]{1,0:T(8,128)(2,1)S(1)} %get-tuple-element.12.refs_0_), channel_id=1, source_target_pairs={{0,4},{1,5},{2,6},{3,7},{8,12},{9,13},{10,14},{11,15},{16,20},{17,... | collective-permute-start | bytes 393224 | tf_op jit(solution)/shard_map/ppermute | solution.py:300
  8.3 3.5 %collective-permute-start.10 = (bf16[128,512]{1,0:T(8,128)(2,1)S(1)}, bf16[128,512]{1,0:T(8,128)(2,1)S(1)}, u32[]{:S(2)}, u32[]{:S(2)}) collective-permute-start(bf16[128,512]{1,0:T(8,128)(2,1)S(1)} %get-tuple-element.12.refs_0_), channel_id=1, source_target_pairs={{0,2},{1,3},{2,4},{3,5},{4,6},{5,7},{8,10},{9,11},{10,12},{11,13},... | collective-permute-start | bytes 393224 | tf_op jit(solution)/shard_map/ppermute | solution.py:300
  11.8 0.1 collective-permute-start
  11.8 1.3 %collective-permute-done.other_owner_ref = s32[1,128]{1,0:T(1,128)S(1)} collective-permute-done((s32[1,128]{1,0:T(1,128)}, s32[1,128]{1,0:T(1,128)S(1)}, u32[]{:S(2)}, u32[]{:S(2)}) %collective-permute-start) | collective-permute-done | bytes 544 | tf_op jit(solution)/shard_map/ppermute | solution.py:300
  13.1 1.9 %collective-permute-start.3 = (bf16[128,512]{1,0:T(8,128)(2,1)S(1)}, bf16[128,512]{1,0:T(8,128)(2,1)S(1)}, u32[]{:S(2)}, u32[]{:S(2)}) collective-permute-start(bf16[128,512]{1,0:T(8,128)(2,1)S(1)} %get-tuple-element.11.refs_0_.refs_6_), channel_id=1, source_target_pairs={{0,2},{1,3},{2,4},{3,5},{4,6},{5,7},{8,10},{9,11},{10,12},{11,13},... | collective-permute-start | bytes 393224 | tf_op jit(solution)/shard_map/ppermute | solution.py:300
  15.0 0.0 collective-permute-done.5.refs_4_.refs_10_
  15.1 0.1 collective-permute-start.9
  15.1 0.0 collective-permute-done.12.refs_4_
  15.1 0.5 collective-permute-start.13
  15.6 0.9 %collective-permute-done.10.refs_2_ = bf16[128,512]{1,0:T(8,128)(2,1)S(1)} collective-permute-done((bf16[128,512]{1,0:T(8,128)(2,1)S(1)}, bf16[128,512]{1,0:T(8,128)(2,1)S(1)}, u32[]{:S(2)}, u32[]{:S(2)}) %collective-permute-start.10) | collective-permute-done | bytes 131104 | tf_op jit(solution)/shard_map/ppermute | solution.py:300
  16.5 0.0 collective-permute-start.11
  16.5 2.3 %collective-permute-done.3.refs_2_.refs_8_ = bf16[128,512]{1,0:T(8,128)(2,1)S(1)} collective-permute-done((bf16[128,512]{1,0:T(8,128)(2,1)S(1)}, bf16[128,512]{1,0:T(8,128)(2,1)S(1)}, u32[]{:S(2)}, u32[]{:S(2)}) %collective-permute-start.3) | collective-permute-done | bytes 131104 | tf_op jit(solution)/shard_map/ppermute | solution.py:300
  18.8 0.0 collective-permute-start.2
  18.8 0.0 collective-permute-done.9.refs_1_
  18.8 0.5 collective-permute-start.6
  19.4 0.0 collective-permute-done.1.other_q_ref
  19.4 0.1 collective-permute-start.4
  19.4 2.2 %order.1 = (f32[32,192,128]{2,1,0:T(8,128)S(1)}, s32[192,128]{1,0:T(8,128)S(1)}) custom-call(s32[1]{0:T(128)} %bitcast.at_ref, s32[8]{0:T(128)} %doc_ref.1, s32[1,128]{1,0:T(1,128)} %bitcast.4, bf16[128,4096]{1,0:T(8,128)(2,1)} %q_ref.1, s32[1,128]{1,0:T(1,128)S(1)} %collective-permute-done.other_owner_ref, ...), custom_call_target="tpu_custom_call" | custom-call | flops 402653184 | bytes 4718592 | tf_op jit(solution)/shard_map/order/pallas_call | solution.py:345
  21.7 0.0 collective-permute-done.13.refs_5_
  21.7 0.0 collective-permute-done.11.refs_3_
  21.7 1.7 %attend.9 = bf16[48,2048]{1,0:T(8,128)(2,1)S(1)} custom-call(s32[1]{0:T(128)} %bitcast.at_ref, f32[32,192,128]{2,1,0:T(8,128)S(1)} %get-tuple-element.9.qs_ref, s32[192,128]{1,0:T(8,128)S(1)} %get-tuple-element.10.info_ref, bf16[128,512]{1,0:T(8,128)(2,1)S(1)} %get-tuple-element.12.refs_0_, bf16[128,512]{1,0:T(8,128)(2,1)S(1)} %collective-permute-done.9.refs_1_, ...), custom_call_target="tpu_custom_call" | custom-call | flops 301989888 | bytes 1376256 | tf_op jit(solution)/shard_map/attend/pallas_call | solution.py:357
  23.4 9.1 %collective-permute-start.14 = (bf16[48,2048]{1,0:T(8,128)(2,1)S(1)}, bf16[48,2048]{1,0:T(8,128)(2,1)S(1)}, u32[]{:S(2)}, u32[]{:S(2)}) collective-permute-start(bf16[48,2048]{1,0:T(8,128)(2,1)S(1)} %attend.9), channel_id=1, source_target_pairs={{0,4},{1,5},{2,6},{3,7},{4,0},{5,1},{6,2},{7,3},{8,12},{9,13},{10,... | collective-permute-start | bytes 589832 | tf_op jit(solution)/shard_map/ppermute | solution.py:300
  32.4 0.0 collective-permute-done.2.refs_1_.refs_7_
  32.4 0.0 collective-permute-done.6.refs_5_.refs_11_
  32.4 0.0 collective-permute-done.4.refs_3_.refs_9_
  32.4 1.7 %attend.7 = bf16[48,2048]{1,0:T(8,128)(2,1)S(1)} custom-call(s32[1]{0:T(128)} %bitcast.at_ref, f32[32,192,128]{2,1,0:T(8,128)S(1)} %get-tuple-element.9.qs_ref, s32[192,128]{1,0:T(8,128)S(1)} %get-tuple-element.10.info_ref, bf16[128,512]{1,0:T(8,128)(2,1)S(1)} %get-tuple-element.11.refs_0_.refs_6_, ...), custom_call_target="tpu_custom_call" | custom-call | flops 301989888 | bytes 1376256 | tf_op jit(solution)/shard_map/attend/pallas_call | solution.py:357
  34.1 0.1 collective-permute-start.7
  34.2 1.7 %attend.10 = bf16[48,2048]{1,0:T(8,128)(2,1)S(1)} custom-call(s32[1]{0:T(128)} %bitcast.at_ref, f32[32,192,128]{2,1,0:T(8,128)S(1)} %get-tuple-element.9.qs_ref, s32[192,128]{1,0:T(8,128)S(1)} %get-tuple-element.10.info_ref, bf16[128,512]{1,0:T(8,128)(2,1)S(1)} %get-tuple-element.12.refs_0_, bf16[128,512]{1,0:T(8,128)(2,1)S(1)} %collective-permute-done.9.refs_1_, ...), custom_call_target="tpu_custom_call" | custom-call | flops 301989888 | bytes 1376256 | tf_op jit(solution)/shard_map/attend/pallas_call | solution.py:357
  35.9 0.6 collective-permute-start.15
  36.5 1.7 %attend.11 = bf16[48,2048]{1,0:T(8,128)(2,1)S(1)} custom-call(s32[1]{0:T(128)} %bitcast.at_ref, f32[32,192,128]{2,1,0:T(8,128)S(1)} %get-tuple-element.9.qs_ref, s32[192,128]{1,0:T(8,128)S(1)} %get-tuple-element.10.info_ref, bf16[128,512]{1,0:T(8,128)(2,1)S(1)} %get-tuple-element.12.refs_0_, bf16[128,512]{1,0:T(8,128)(2,1)S(1)} %collective-permute-done.9.refs_1_, ...), custom_call_target="tpu_custom_call" | custom-call | flops 301989888 | bytes 1376256 | tf_op jit(solution)/shard_map/attend/pallas_call | solution.py:357
  38.1 3.3 %collective-permute-start.16 = (bf16[48,2048]{1,0:T(8,128)(2,1)S(1)}, bf16[48,2048]{1,0:T(8,128)(2,1)S(1)}, u32[]{:S(2)}, u32[]{:S(2)}) collective-permute-start(bf16[48,2048]{1,0:T(8,128)(2,1)S(1)} %attend.11), channel_id=1, source_target_pairs={{0,6},{1,7},{2,0},{3,1},{4,2},{5,3},{6,4},{7,5},{8,14},{9,15},{10,... | collective-permute-start | bytes 589832 | tf_op jit(solution)/shard_map/ppermute | solution.py:300
  41.5 1.7 %attend.12 = bf16[48,2048]{1,0:T(8,128)(2,1)S(1)} custom-call(s32[1]{0:T(128)} %bitcast.at_ref, f32[32,192,128]{2,1,0:T(8,128)S(1)} %get-tuple-element.9.qs_ref, s32[192,128]{1,0:T(8,128)S(1)} %get-tuple-element.10.info_ref, bf16[128,512]{1,0:T(8,128)(2,1)S(1)} %get-tuple-element.11.refs_0_.refs_6_, ...), custom_call_target="tpu_custom_call" | custom-call | flops 301989888 | bytes 1376256 | tf_op jit(solution)/shard_map/attend/pallas_call | solution.py:357
  43.1 0.6 collective-permute-start.17
  43.7 1.7 %attend.8 = bf16[48,2048]{1,0:T(8,128)(2,1)S(1)} custom-call(s32[1]{0:T(128)} %bitcast.at_ref, f32[32,192,128]{2,1,0:T(8,128)S(1)} %get-tuple-element.9.qs_ref, s32[192,128]{1,0:T(8,128)S(1)} %get-tuple-element.10.info_ref, bf16[128,512]{1,0:T(8,128)(2,1)S(1)} %get-tuple-element.11.refs_0_.refs_6_, ...), custom_call_target="tpu_custom_call" | custom-call | flops 301989888 | bytes 1376256 | tf_op jit(solution)/shard_map/attend/pallas_call | solution.py:357
  45.4 5.7 %collective-permute-done.14.refs_0_ = bf16[48,2048]{1,0:T(8,128)(2,1)S(1)} collective-permute-done((bf16[48,2048]{1,0:T(8,128)(2,1)S(1)}, bf16[48,2048]{1,0:T(8,128)(2,1)S(1)}, u32[]{:S(2)}, u32[]{:S(2)}) %collective-permute-start.14) | collective-permute-done | bytes 196640 | tf_op jit(solution)/shard_map/ppermute | solution.py:300
  51.1 0.0 collective-permute-start.8
  51.1 2.7 %attend.13.refs_4_ = bf16[48,4096]{1,0:T(8,128)(2,1)S(1)} custom-call(s32[1]{0:T(128)} %bitcast.at_ref, f32[32,192,128]{2,1,0:T(8,128)S(1)} %get-tuple-element.9.qs_ref, s32[192,128]{1,0:T(8,128)S(1)} %get-tuple-element.10.info_ref, bf16[128,512]{1,0:T(8,128)(2,1)S(1)} %get-tuple-element.12.refs_0_, bf16[128,512]{1,0:T(8,128)(2,1)S(1)} %collective-permute-done.9.refs_1_, ...), custom_call_target="tpu_custom_call" | custom-call | flops 603979776 | bytes 2752512 | tf_op jit(solution)/shard_map/attend/pallas_call | solution.py:357
  53.7 0.0 collective-permute-done.15.refs_1_
  53.8 1.1 %collective-permute-done.16.refs_2_ = bf16[48,2048]{1,0:T(8,128)(2,1)S(1)} collective-permute-done((bf16[48,2048]{1,0:T(8,128)(2,1)S(1)}, bf16[48,2048]{1,0:T(8,128)(2,1)S(1)}, u32[]{:S(2)}, u32[]{:S(2)}) %collective-permute-start.16) | collective-permute-done | bytes 196640 | tf_op jit(solution)/shard_map/ppermute | solution.py:300
  54.9 8.6 %collective-permute-done.17.refs_3_ = bf16[48,2048]{1,0:T(8,128)(2,1)S(1)} collective-permute-done((bf16[48,2048]{1,0:T(8,128)(2,1)S(1)}, bf16[48,2048]{1,0:T(8,128)(2,1)S(1)}, u32[]{:S(2)}, u32[]{:S(2)}) %collective-permute-start.17) | collective-permute-done | bytes 196640 | tf_op jit(solution)/shard_map/ppermute | solution.py:300
  63.5 1.0 %lay.2.refs_2_ = bf16[4,48,4096]{2,1,0:T(8,128)(2,1)} custom-call(s32[1]{0:T(128)} %bitcast.at_ref, bf16[48,2048]{1,0:T(8,128)(2,1)S(1)} %collective-permute-done.14.refs_0_, bf16[48,2048]{1,0:T(8,128)(2,1)S(1)} %collective-permute-done.15.refs_1_, bf16[48,2048]{1,0:T(8,128)(2,1)S(1)} %collective-permute-done.16.refs_2_, ...), custom_call_target="tpu_custom_call" | custom-call | bytes 3145728 | tf_op jit(solution)/shard_map/lay/pallas_call | solution.py:384
  64.6 0.0 collective-permute-done.7.refs_0_
  64.6 0.0 collective-permute-done.8.refs_1_
  64.6 0.8 %lay.3 = bf16[4,48,4096]{2,1,0:T(8,128)(2,1)} custom-call(s32[1]{0:T(128)} %bitcast.at_ref, bf16[48,2048]{1,0:T(8,128)(2,1)S(1)} %collective-permute-done.7.refs_0_, bf16[48,2048]{1,0:T(8,128)(2,1)S(1)} %collective-permute-done.8.refs_1_, bf16[4,48,4096]{2,1,0:T(8,128)(2,1)} %lay.2.refs_2_), custom_call_target="tpu_custom_call", output_to_operand_aliasing={{}: (3, {})} | custom-call | bytes 3145728 | tf_op jit(solution)/shard_map/lay/pallas_call | solution.py:384
Async XLA Ops:
  0.0 19.4 %collective-permute-start.1 = (bf16[128,4096]{1,0:T(8,128)(2,1)}, bf16[128,4096]{1,0:T(8,128)(2,1)S(1)}, u32[]{:S(2)}, u32[]{:S(2)}) collective-permute-start(bf16[128,4096]{1,0:T(8,128)(2,1)} %q_ref.1), channel_id=1, source_target_pairs={{0,1},{1,0},{2,3},{3,2},{4,5},{5,4},{6,7},{7,6},{8,9},{9,8},{10,11... | collective-permute-start | bytes 3145736 | tf_op jit(solution)/shard_map/ppermute | solution.py:300
  1.5 13.6 %collective-permute-start.5 = (bf16[128,512]{1,0:T(8,128)(2,1)S(1)}, bf16[128,512]{1,0:T(8,128)(2,1)S(1)}, u32[]{:S(2)}, u32[]{:S(2)}) collective-permute-start(bf16[128,512]{1,0:T(8,128)(2,1)S(1)} %get-tuple-element.11.refs_0_.refs_6_), channel_id=1, source_target_pairs={{0,4},{1,5},{2,6},{3,7},{8,12},{9,13},{10,14},{11,15},{16,20},{17,... | collective-permute-start | bytes 393224 | tf_op jit(solution)/shard_map/ppermute | solution.py:300
  7.0 8.2 %collective-permute-start.12 = (bf16[128,512]{1,0:T(8,128)(2,1)S(1)}, bf16[128,512]{1,0:T(8,128)(2,1)S(1)}, u32[]{:S(2)}, u32[]{:S(2)}) collective-permute-start(bf16[128,512]{1,0:T(8,128)(2,1)S(1)} %get-tuple-element.12.refs_0_), channel_id=1, source_target_pairs={{0,4},{1,5},{2,6},{3,7},{8,12},{9,13},{10,14},{11,15},{16,20},{17,... | collective-permute-start | bytes 393224 | tf_op jit(solution)/shard_map/ppermute | solution.py:300
  8.3 8.2 %collective-permute-start.10 = (bf16[128,512]{1,0:T(8,128)(2,1)S(1)}, bf16[128,512]{1,0:T(8,128)(2,1)S(1)}, u32[]{:S(2)}, u32[]{:S(2)}) collective-permute-start(bf16[128,512]{1,0:T(8,128)(2,1)S(1)} %get-tuple-element.12.refs_0_), channel_id=1, source_target_pairs={{0,2},{1,3},{2,4},{3,5},{4,6},{5,7},{8,10},{9,11},{10,12},{11,13},... | collective-permute-start | bytes 393224 | tf_op jit(solution)/shard_map/ppermute | solution.py:300
  11.8 1.4 %collective-permute-start = (s32[1,128]{1,0:T(1,128)}, s32[1,128]{1,0:T(1,128)S(1)}, u32[]{:S(2)}, u32[]{:S(2)}) collective-permute-start(s32[1,128]{1,0:T(1,128)} %bitcast.3), channel_id=1, source_target_pairs={{0,1},{1,0},{2,3},{3,2},{4,5},{5,4},{6,7},{7,6},{8,9},{9,8},{10,11... | collective-permute-start | bytes 1544 | tf_op jit(solution)/shard_map/ppermute | solution.py:300
  13.1 5.7 %collective-permute-start.3 = (bf16[128,512]{1,0:T(8,128)(2,1)S(1)}, bf16[128,512]{1,0:T(8,128)(2,1)S(1)}, u32[]{:S(2)}, u32[]{:S(2)}) collective-permute-start(bf16[128,512]{1,0:T(8,128)(2,1)S(1)} %get-tuple-element.11.refs_0_.refs_6_), channel_id=1, source_target_pairs={{0,2},{1,3},{2,4},{3,5},{4,6},{5,7},{8,10},{9,11},{10,12},{11,13},... | collective-permute-start | bytes 393224 | tf_op jit(solution)/shard_map/ppermute | solution.py:300
  15.1 3.8 %collective-permute-start.9 = (bf16[128,512]{1,0:T(8,128)(2,1)S(1)}, bf16[128,512]{1,0:T(8,128)(2,1)S(1)}, u32[]{:S(2)}, u32[]{:S(2)}) collective-permute-start(bf16[128,512]{1,0:T(8,128)(2,1)S(1)} %get-tuple-element.12.refs_0_), channel_id=1, source_target_pairs={{0,1},{1,0},{2,3},{3,2},{4,5},{5,4},{6,7},{7,6},{8,9},{9,8},{10,11... | collective-permute-start | bytes 393224 | tf_op jit(solution)/shard_map/ppermute | solution.py:300
  15.1 6.5 %collective-permute-start.13 = (bf16[128,512]{1,0:T(8,128)(2,1)S(1)}, bf16[128,512]{1,0:T(8,128)(2,1)S(1)}, u32[]{:S(2)}, u32[]{:S(2)}) collective-permute-start(bf16[128,512]{1,0:T(8,128)(2,1)S(1)} %collective-permute-done.12.refs_4_), channel_id=1, source_target_pairs={{0,1},{1,0},{2,3},{3,2},{4,5},{5,4},{6,7},{7,6},{8,9},{9,8},{10,11... | collective-permute-start | bytes 393224 | tf_op jit(solution)/shard_map/ppermute | solution.py:300
  16.5 5.2 %collective-permute-start.11 = (bf16[128,512]{1,0:T(8,128)(2,1)S(1)}, bf16[128,512]{1,0:T(8,128)(2,1)S(1)}, u32[]{:S(2)}, u32[]{:S(2)}) collective-permute-start(bf16[128,512]{1,0:T(8,128)(2,1)S(1)} %collective-permute-done.10.refs_2_), channel_id=1, source_target_pairs={{0,1},{1,0},{2,3},{3,2},{4,5},{5,4},{6,7},{7,6},{8,9},{9,8},{10,11... | collective-permute-start | bytes 393224 | tf_op jit(solution)/shard_map/ppermute | solution.py:300
  18.8 13.6 %collective-permute-start.2 = (bf16[128,512]{1,0:T(8,128)(2,1)S(1)}, bf16[128,512]{1,0:T(8,128)(2,1)S(1)}, u32[]{:S(2)}, u32[]{:S(2)}) collective-permute-start(bf16[128,512]{1,0:T(8,128)(2,1)S(1)} %get-tuple-element.11.refs_0_.refs_6_), channel_id=1, source_target_pairs={{0,1},{1,0},{2,3},{3,2},{4,5},{5,4},{6,7},{7,6},{8,9},{9,8},{10,11... | collective-permute-start | bytes 393224 | tf_op jit(solution)/shard_map/ppermute | solution.py:300
  18.8 13.6 %collective-permute-start.6 = (bf16[128,512]{1,0:T(8,128)(2,1)S(1)}, bf16[128,512]{1,0:T(8,128)(2,1)S(1)}, u32[]{:S(2)}, u32[]{:S(2)}) collective-permute-start(bf16[128,512]{1,0:T(8,128)(2,1)S(1)} %collective-permute-done.5.refs_4_.refs_10_), channel_id=1, source_target_pairs={{0,1},{1,0},{2,3},{3,2},{4,5},{5,4},{6,7},{7,6},{8,9},{9,8},{10,11... | collective-permute-start | bytes 393224 | tf_op jit(solution)/shard_map/ppermute | solution.py:300
  19.4 13.1 %collective-permute-start.4 = (bf16[128,512]{1,0:T(8,128)(2,1)S(1)}, bf16[128,512]{1,0:T(8,128)(2,1)S(1)}, u32[]{:S(2)}, u32[]{:S(2)}) collective-permute-start(bf16[128,512]{1,0:T(8,128)(2,1)S(1)} %collective-permute-done.3.refs_2_.refs_8_), channel_id=1, source_target_pairs={{0,1},{1,0},{2,3},{3,2},{4,5},{5,4},{6,7},{7,6},{8,9},{9,8},{10,11... | collective-permute-start | bytes 393224 | tf_op jit(solution)/shard_map/ppermute | solution.py:300
  23.4 27.7 %collective-permute-start.14 = (bf16[48,2048]{1,0:T(8,128)(2,1)S(1)}, bf16[48,2048]{1,0:T(8,128)(2,1)S(1)}, u32[]{:S(2)}, u32[]{:S(2)}) collective-permute-start(bf16[48,2048]{1,0:T(8,128)(2,1)S(1)} %attend.9), channel_id=1, source_target_pairs={{0,4},{1,5},{2,6},{3,7},{4,0},{5,1},{6,2},{7,3},{8,12},{9,13},{10,... | collective-permute-start | bytes 589832 | tf_op jit(solution)/shard_map/ppermute | solution.py:300
  34.1 30.4 %collective-permute-start.7 = (bf16[48,2048]{1,0:T(8,128)(2,1)S(1)}, bf16[48,2048]{1,0:T(8,128)(2,1)S(1)}, u32[]{:S(2)}, u32[]{:S(2)}) collective-permute-start(bf16[48,2048]{1,0:T(8,128)(2,1)S(1)} %attend.7), channel_id=1, source_target_pairs={{0,2},{1,3},{2,4},{3,5},{4,6},{5,7},{6,0},{7,1},{8,10},{9,11},{10,... | collective-permute-start | bytes 589832 | tf_op jit(solution)/shard_map/ppermute | solution.py:300
  35.9 17.9 %collective-permute-start.15 = (bf16[48,2048]{1,0:T(8,128)(2,1)S(1)}, bf16[48,2048]{1,0:T(8,128)(2,1)S(1)}, u32[]{:S(2)}, u32[]{:S(2)}) collective-permute-start(bf16[48,2048]{1,0:T(8,128)(2,1)S(1)} %attend.10), channel_id=1, source_target_pairs={{0,2},{1,3},{2,4},{3,5},{4,6},{5,7},{6,0},{7,1},{8,10},{9,11},{10,... | collective-permute-start | bytes 589832 | tf_op jit(solution)/shard_map/ppermute | solution.py:300
  38.1 16.7 %collective-permute-start.16 = (bf16[48,2048]{1,0:T(8,128)(2,1)S(1)}, bf16[48,2048]{1,0:T(8,128)(2,1)S(1)}, u32[]{:S(2)}, u32[]{:S(2)}) collective-permute-start(bf16[48,2048]{1,0:T(8,128)(2,1)S(1)} %attend.11), channel_id=1, source_target_pairs={{0,6},{1,7},{2,0},{3,1},{4,2},{5,3},{6,4},{7,5},{8,14},{9,15},{10,... | collective-permute-start | bytes 589832 | tf_op jit(solution)/shard_map/ppermute | solution.py:300
  43.1 20.4 %collective-permute-start.17 = (bf16[48,2048]{1,0:T(8,128)(2,1)S(1)}, bf16[48,2048]{1,0:T(8,128)(2,1)S(1)}, u32[]{:S(2)}, u32[]{:S(2)}) collective-permute-start(bf16[48,2048]{1,0:T(8,128)(2,1)S(1)} %attend.12), channel_id=1, source_target_pairs={{0,4},{1,5},{2,6},{3,7},{4,0},{5,1},{6,2},{7,3},{8,12},{9,13},{10,... | collective-permute-start | bytes 589832 | tf_op jit(solution)/shard_map/ppermute | solution.py:300
  51.1 13.5 %collective-permute-start.8 = (bf16[48,2048]{1,0:T(8,128)(2,1)S(1)}, bf16[48,2048]{1,0:T(8,128)(2,1)S(1)}, u32[]{:S(2)}, u32[]{:S(2)}) collective-permute-start(bf16[48,2048]{1,0:T(8,128)(2,1)S(1)} %attend.8), channel_id=1, source_target_pairs={{0,6},{1,7},{2,0},{3,1},{4,2},{5,3},{6,4},{7,5},{8,14},{9,15},{10,... | collective-permute-start | bytes 589832 | tf_op jit(solution)/shard_map/ppermute | solution.py:300
